TPU v7x, 32 devices: a whole 2x2x4 slice. The times are simulated.
32 devices in a mesh: hi: 4 (over z), lo: 8 (over y, x, core).
Axes of the slice: x: 2, y: 2, z: 4, core: 2. Of those that a mesh axis runs over, the one named last changes fastest.
Arguments:
- state: float32 [2, 33554432], P(None, ('hi', 'lo')), may hold values from -6 to 6
Outputs:
- transformed: float32 [2, 33554432], P(None, ('hi', 'lo'))
All inputs are finite; a program needn't handle non-finite values.
Results may differ from a plain program's by a relative error of at most 0.0003.
Values sent between devices are 32-bit elements.
A program may use at most 128 MiB of HBM per device.

v0:
```python
import math
import jax
import jax.numpy as jnp
from jax import lax
from jax.sharding import PartitionSpec as P

SUB_A = 1024


def product(left, right):
    return jnp.dot(left, right, precision=lax.Precision.HIGHEST, preferred_element_type=jnp.float32)


def dft_table(length, factor):
    steps = jnp.arange(length, dtype=jnp.int32)
    indices = steps[:, None] * steps[None, :] % length
    phases = indices.astype(jnp.float32) * (2.0 * math.pi / length)
    return (jnp.cos(phases) * factor, jnp.sin(phases) * factor)


def rotate(real_part, imag_part, phases):
    cosine = jnp.cos(phases)
    sine = jnp.sin(phases)
    return (real_part * cosine - imag_part * sine, real_part * sine + imag_part * cosine)


def remap_entry(blocks):
    return lax.all_to_all(blocks, ("hi", "lo"), split_axis=1, concat_axis=1, tiled=True)


def remap_middle(blocks):
    return lax.all_to_all(blocks, ("hi", "lo"), split_axis=1, concat_axis=1, tiled=True)


def remap_final(blocks):
    return lax.all_to_all(blocks, ("hi", "lo"), split_axis=1, concat_axis=1, tiled=True)


def shards(state):
    count_high = lax.axis_size("hi")
    count_low = lax.axis_size("lo")
    devices_all = count_high * count_low
    device_pos = lax.axis_index("hi") * count_low + lax.axis_index("lo")
    amplitudes = state.shape[1]
    per_peer = amplitudes // devices_all
    whole_size = amplitudes * devices_all
    blocks = remap_entry(state.reshape(2, devices_all, per_peer))
    table_re, table_im = dft_table(devices_all, 1.0 / math.sqrt(devices_all))
    mixed_re = product(table_re, blocks[0]) - product(table_im, blocks[1])
    mixed_im = product(table_re, blocks[1]) + product(table_im, blocks[0])
    row_ids = jnp.arange(devices_all, dtype=jnp.int32)
    col_ids = device_pos * per_peer + jnp.arange(per_peer, dtype=jnp.int32)
    phases = (row_ids[:, None] * col_ids[None, :] % whole_size).astype(jnp.float32) * (
        2.0 * math.pi / whole_size
    )
    mixed_re, mixed_im = rotate(mixed_re, mixed_im, phases)
    gathered = remap_middle(jnp.stack([mixed_re, mixed_im]))
    outer_len = SUB_A
    inner_len = amplitudes // outer_len
    local_grid = gathered.reshape(2, outer_len, inner_len)
    outer_re, outer_im = dft_table(outer_len, 1.0 / math.sqrt(outer_len))
    half_re = product(outer_re, local_grid[0]) - product(outer_im, local_grid[1])
    half_im = product(outer_re, local_grid[1]) + product(outer_im, local_grid[0])
    outer_ids = jnp.arange(outer_len, dtype=jnp.int32)
    inner_ids = jnp.arange(inner_len, dtype=jnp.int32)
    phases = (outer_ids[:, None] * inner_ids[None, :] % amplitudes).astype(jnp.float32) * (
        2.0 * math.pi / amplitudes
    )
    half_re, half_im = rotate(half_re, half_im, phases)
    inner_re, inner_im = dft_table(inner_len, 1.0 / math.sqrt(inner_len))
    done_re = product(half_re, inner_re) - product(half_im, inner_im)
    done_im = product(half_re, inner_im) + product(half_im, inner_re)
    ordered = jnp.stack([done_re, done_im]).transpose(0, 2, 1).reshape(2, devices_all, per_peer)
    arrived = remap_final(ordered)
    return arrived.transpose(0, 2, 1).reshape(2, amplitudes)


def solution(mesh):
    placed = (P(None, ("hi", "lo")),)
    return jax.shard_map(
        shards, mesh=mesh, in_specs=placed, out_specs=P(None, ("hi", "lo")), check_vma=False
    )
```

profile of v0, /device:TPU:0, one launch (start us, length us, event | category | flops | bytes accessed | tf_op | source)
XLA Modules:
  0.0 1071.1 jit_solution(11624295385155374427)
XLA Ops:
  0.0 7.5 all-to-all-start
  7.5 185.9 %all-to-all-done = f32[2,32,32768]{2,0,1:T(2,128)} async-done(((f32[2,32,32768]{2,0,1:T(2,128)}), f32[2,32,32768]{2,0,1:T(2,128)}, u32[]{:S(2)}, u32[]{:S(2)}) %all-to-all-start) | async-done | bytes 8388640 | tf_op jit(solution)/shard_map/all_to_all | solution.py:28
  193.4 9.9 fusion.143
  203.2 5.9 fusion.11
  209.1 5.9 fusion.7
  215.0 6.1 convolution_add_fusion
  221.1 22.9 %subtract_bitcast_fusion.1 = (f32[1,32,32768]{2,1,0:T(8,128)S(1)}, f32[1,32,32768]{2,1,0:T(8,128)S(1)}) fusion(f32[32,32768]{1,0:T(8,128)S(1)} %convolution_add_fusion, s32[32768]{0:T(1024)S(1)} %iota_add_fusion, f32[32,32768]{1,0:T(8,128)S(1)} %fusion.11, f32[1,32,32768]{2,0,1:T(1,128)S(1)} %get-tuple-element.10), kind=kOutput, calls=%fused_computation.33 | convolution fusion | flops 424688640 | bytes 21102592 | tf_op jit(solution)/shard_map/dot_general | solution.py:11
  244.1 0.5 pad_maximum_fusion
  244.6 14.3 %copy.4 = f32[2,32,32768]{2,0,1:T(2,128)S(1)} copy(f32[2,32,32768]{2,1,0:T(8,128)S(1)} %pad_maximum_fusion) | data formatting | bytes 16777216 | tf_op jit(solution)/shard_map/stack | solution.py:57
  258.9 186.0 %all_to_all.15 = f32[2,32,32768]{2,0,1:T(2,128)} all-to-all(f32[2,32,32768]{2,0,1:T(2,128)S(1)} %copy.4), channel_id=1, replica_groups=mesh['hi'=4,'lo'=8] {'hi','lo'}, dimensions={1} | all-to-all | bytes 16777216 | tf_op jit(solution)/shard_map/all_to_all | solution.py:32
  444.9 28.8 %slice_reduce_fusion.1 = (f32[32,32768]{1,0:T(8,128)}, f32[32,32768]{1,0:T(8,128)}) fusion(f32[2,32,32768]{2,0,1:T(2,128)} %all_to_all.15), kind=kLoop, calls=%fused_computation.20 | loop fusion | bytes 16777216 | tf_op jit(solution)/shard_map/slice | solution.py:62
  473.7 4.9 squeeze.18
  478.7 4.9 squeeze.19
  483.6 0.0 copy-start
  483.6 31.5 %fusion.29 = f32[1024,1024]{1,0:T(8,128)S(1)} fusion(f32[1024,1024]{1,0:T(8,128)} %squeeze.19), kind=kOutput, calls=%fused_computation.52 | convolution fusion | flops 12900630528 | bytes 8388608 | tf_op jit(solution)/shard_map/dot_general | solution.py:11
  515.2 0.0 copy-done
  515.2 29.6 %fusion.30 = f32[1024,1024]{1,0:T(8,128)S(1)} fusion(f32[1024,1024]{1,0:T(8,128)S(1)} %copy-done), kind=kOutput, calls=%fused_computation.53 | convolution fusion | flops 12900630528 | bytes 8388608 | tf_op jit(solution)/shard_map/dot_general | solution.py:11
  544.8 0.0 copy-start.1
  544.8 29.2 %fusion.56 = f32[1024,1024]{1,0:T(8,128)S(1)} fusion(f32[1024,1024]{1,0:T(8,128)S(1)} %fusion.29, f32[1024,1024]{1,0:T(8,128)S(1)} %copy-done), kind=kOutput, calls=%fused_computation.71 | convolution fusion | flops 12901679104 | bytes 12582912 | tf_op jit(solution)/shard_map/dot_general | solution.py:11
  574.0 0.0 copy-done.1
  574.0 29.7 %fusion.55 = f32[1024,1024]{1,0:T(8,128)S(1)} fusion(f32[1024,1024]{1,0:T(8,128)S(1)} %fusion.30, f32[1024,1024]{1,0:T(8,128)S(1)} %copy-done.1), kind=kOutput, calls=%fused_computation.70 | convolution fusion | flops 12901679104 | bytes 12582912 | tf_op jit(solution)/shard_map/dot_general | solution.py:11
  603.7 16.8 %multiply_add_fusion.10 = f32[1024,1024]{1,0:T(8,128)S(1)} fusion(f32[1024,1024]{1,0:T(8,128)S(1)} %fusion.56, f32[1024,1024]{1,0:T(8,128)S(1)} %fusion.55), kind=kLoop, calls=%fused_computation.29.clone.clone.2 | loop fusion | flops 17825792 | bytes 12582912 | tf_op jit(solution)/shard_map/dot_general | solution.py:11
  620.6 16.8 %multiply_subtract_fusion.9 = f32[1024,1024]{1,0:T(8,128)S(1)} fusion(f32[1024,1024]{1,0:T(8,128)S(1)} %fusion.56, f32[1024,1024]{1,0:T(8,128)S(1)} %fusion.55), kind=kLoop, calls=%fused_computation.30.clone.clone.2 | loop fusion | flops 17825792 | bytes 12582912 | tf_op jit(solution)/shard_map/dot_general | solution.py:11
  637.4 16.8 %multiply_add_fusion.9 = f32[1024,1024]{1,0:T(8,128)S(1)} fusion(f32[1024,1024]{1,0:T(8,128)S(1)} %fusion.56, f32[1024,1024]{1,0:T(8,128)S(1)} %fusion.55), kind=kLoop, calls=%fused_computation.29.clone.1.clone.2 | loop fusion | flops 17825792 | bytes 12582912 | tf_op jit(solution)/shard_map/dot_general | solution.py:11
  654.2 16.8 %multiply_subtract_fusion.10 = f32[1024,1024]{1,0:T(8,128)S(1)} fusion(f32[1024,1024]{1,0:T(8,128)S(1)} %fusion.56, f32[1024,1024]{1,0:T(8,128)S(1)} %fusion.55), kind=kLoop, calls=%fused_computation.30.clone.1.clone.2 | loop fusion | flops 17825792 | bytes 12582912 | tf_op jit(solution)/shard_map/dot_general | solution.py:11
  671.1 31.3 %fusion.27 = f32[1024,1024]{1,0:T(8,128)S(1)} fusion(f32[1024,1024]{1,0:T(8,128)S(1)} %multiply_add_fusion.10), kind=kOutput, calls=%fused_computation.50 | convolution fusion | flops 12900630528 | bytes 8388608 | tf_op jit(solution)/shard_map/dot_general | solution.py:11
  702.4 31.4 %fusion.28 = f32[1024,1024]{1,0:T(8,128)S(1)} fusion(f32[1024,1024]{1,0:T(8,128)S(1)} %multiply_subtract_fusion.10), kind=kOutput, calls=%fused_computation.51 | convolution fusion | flops 12900630528 | bytes 8388608 | tf_op jit(solution)/shard_map/dot_general | solution.py:11
  733.8 31.5 %add_bitcast_fusion = f32[1,1024,1024]{2,1,0:T(8,128)S(1)} fusion(f32[1024,1024]{1,0:T(8,128)S(1)} %fusion.27, f32[1024,1024]{1,0:T(8,128)S(1)} %multiply_subtract_fusion.9), kind=kOutput, calls=%fused_computation.27 | convolution fusion | flops 12901679104 | bytes 12582912 | tf_op jit(solution)/shard_map/dot_general | solution.py:11
  765.3 31.3 %subtract_bitcast_fusion = f32[1,1024,1024]{2,1,0:T(8,128)S(1)} fusion(f32[1024,1024]{1,0:T(8,128)S(1)} %fusion.28, f32[1024,1024]{1,0:T(8,128)S(1)} %multiply_add_fusion.9), kind=kOutput, calls=%fused_computation.28 | convolution fusion | flops 12901679104 | bytes 12582912 | tf_op jit(solution)/shard_map/dot_general | solution.py:11
  796.6 4.2 maximum_bitcast_fusion
  800.8 8.7 copy.5
  809.5 9.4 reshape.19
  818.9 14.4 %copy.6 = f32[2,32,32768]{2,0,1:T(2,128)S(1)} copy(f32[2,32,32768]{2,1,0:T(8,128)} %reshape.19) | data formatting | bytes 16777216 | tf_op jit(solution)/shard_map/reshape | solution.py:73
  833.3 187.3 %all_to_all.16 = f32[2,32,32768]{2,0,1:T(2,128)} all-to-all(f32[2,32,32768]{2,0,1:T(2,128)S(1)} %copy.6), channel_id=1, replica_groups=mesh['hi'=4,'lo'=8] {'hi','lo'}, dimensions={1} | all-to-all | bytes 16777216 | tf_op jit(solution)/shard_map/all_to_all | solution.py:36
  1020.6 22.5 %copy.7 = f32[2,32768,32]{2,1,0:T(8,128)} copy(f32[2,32768,32]{1,0,2:T(2,128)} %bitcast.36) | data formatting | bytes 16777216 | tf_op jit(solution)/shard_map/transpose | solution.py:75
  1043.1 27.8 %reshape.20 = f32[2,1048576]{1,0:T(2,128)} reshape(f32[2,32768,32]{2,1,0:T(8,128)} %copy.7) | data formatting | bytes 16777216 | tf_op jit(solution)/shard_map/reshape | solution.py:75
  (1 shorter events, 0.0 us)
Async XLA Ops:
  0.0 193.4 %all-to-all-start = ((f32[2,32,32768]{2,0,1:T(2,128)}), f32[2,32,32768]{2,0,1:T(2,128)}, u32[]{:S(2)}, u32[]{:S(2)}) async-start(f32[2,32,32768]{2,0,1:T(2,128)} %bitcast.37), calls=%async_computation | async-start | bytes 16777216 | tf_op jit(solution)/shard_map/all_to_all | solution.py:28
  483.6 31.6 %copy-start = (f32[1024,1024]{1,0:T(8,128)S(1)}, f32[1024,1024]{1,0:T(8,128)}, u32[]{:S(2)}) copy-start(f32[1024,1024]{1,0:T(8,128)} %squeeze.18) | copy-start | bytes 12582916
  544.8 29.2 %copy-start.1 = (f32[1024,1024]{1,0:T(8,128)S(1)}, f32[1024,1024]{1,0:T(8,128)}, u32[]{:S(2)}) copy-start(f32[1024,1024]{1,0:T(8,128)} %squeeze.19) | copy-start | bytes 12582916
where the time goes:
time: 1080 us; the launch traced here: 1070 us
  blocking collectives  373 us (35%)
  matrix products  286 us (26%)
  waiting for transfers between devices  186 us (17%)
  local copies, waits for them, and re-layouts  146 us (14%)
  other arithmetic  72.1 us (7%)
    dot_general x12, matrix products, product(): jnp.dot(left, right, precision=lax.Precision.HIGHEST, preferred_element_t...  286 us
    all_to_all x1, blocking collectives, remap_final(): lax.all_to_all(blocks, ('hi', 'lo'), split_axis=1, concat_axis=1, tiled=T...  187 us
    all_to_all x1, blocking collectives, remap_middle(): lax.all_to_all(blocks, ('hi', 'lo'), split_axis=1, concat_axis=1, tiled=T...  186 us
    all_to_all x1, waiting for transfers between devices, remap_entry(): lax.all_to_all(blocks, ('hi', 'lo'), split_axis=1, concat_axis=1, tiled=T...  186 us
    dot_general x4, other arithmetic, product(): jnp.dot(left, right, precision=lax.Precision.HIGHEST, preferred_element_t...  67.3 us
    slice x1, local copies, waits for them, and re-layouts, shards(): local_grid[0]  28.8 us
    reshape x1, local copies, waits for them, and re-layouts, shards(): return arrived.transpose(0, 2, 1).reshape(2, amplitudes)  27.8 us
    reshape x2, local copies, waits for them, and re-layouts, shards(): jnp.stack([done_re, done_im]).transpose(0, 2, 1)  23.7 us
  transfers between devices with their start and end apart: 1, of which 1 were waited for; matrix products, arithmetic and copies ran while one was open for 0% of the time, Pallas kernels for 0%

commit v1 on v0

--- a/solution.py
+++ b/solution.py
@@ -5,6 +5,13 @@
 from jax.sharding import PartitionSpec as P
 
 SUB_A = 1024
+
+
+def swap_blocks(block, axis, split, join):
+    n_dev = lax.axis_size(axis)
+    blocks = jnp.stack(jnp.split(block, n_dev, axis=split), axis=0)
+    blocks = lax.all_to_all(blocks, axis, split_axis=0, concat_axis=0)
+    return jnp.concatenate(blocks, axis=join)
 
 
 def product(left, right):
@@ -33,7 +40,7 @@
 
 
 def remap_final(blocks):
-    return lax.all_to_all(blocks, ("hi", "lo"), split_axis=1, concat_axis=1, tiled=True)
+    return swap_blocks(blocks, ("hi", "lo"), 1, 1)
 
 
 def shards(state):

time: 1080 us -> 1130 us (1.046)
  local copies, waits for them, and re-layouts: 146 us -> 198 us
    unnamed x4 -> x36, local copies, waits for them, and re-layouts: 0.01 us -> 64.2 us
    reshape x2 -> x1, local copies, waits for them, and re-layouts: 23.7 us -> 9.54 us  [shards(): jnp.stack([done_re, done_im]).transpose(0, 2, 1)]
where the time goes in v1:
time: 1130 us; the launch traced here: 1120 us
  blocking collectives  373 us (33%)
  matrix products  286 us (25%)
  local copies, waits for them, and re-layouts  198 us (18%)
  waiting for transfers between devices  186 us (16%)
  other arithmetic  72.1 us (6%)
    dot_general x12, matrix products, product(): jnp.dot(left, right, precision=lax.Precision.HIGHEST, preferred_element_t...  286 us
    all_to_all x1, blocking collectives, swap_blocks(): blocks = lax.all_to_all(blocks, axis, split_axis=0, concat_axis=0)  187 us
    all_to_all x1, blocking collectives, remap_middle(): lax.all_to_all(blocks, ('hi', 'lo'), split_axis=1, concat_axis=1, tiled=T...  186 us
    all_to_all x1, waiting for transfers between devices, remap_entry(): lax.all_to_all(blocks, ('hi', 'lo'), split_axis=1, concat_axis=1, tiled=T...  186 us
    dot_general x4, other arithmetic, product(): jnp.dot(left, right, precision=lax.Precision.HIGHEST, preferred_element_t...  67.3 us
    unnamed x36, local copies, waits for them, and re-layouts  64.2 us
    slice x1, local copies, waits for them, and re-layouts, shards(): local_grid[0]  28.8 us
    reshape x1, local copies, waits for them, and re-layouts, shards(): return arrived.transpose(0, 2, 1).reshape(2, amplitudes)  27.8 us
  transfers between devices with their start and end apart: 1, of which 1 were waited for; matrix products, arithmetic and copies ran while one was open for 0% of the time, Pallas kernels for 0%

profile of v1, /device:TPU:0, one launch (start us, length us, event | category | flops | bytes accessed | tf_op | source)
XLA Modules:
  0.0 1123.3 jit_solution(8773333840686247937)
XLA Ops:
  0.0 7.5 all-to-all-start
  7.5 185.9 %all-to-all-done = f32[2,32,32768]{2,0,1:T(2,128)} async-done(((f32[2,32,32768]{2,0,1:T(2,128)}), f32[2,32,32768]{2,0,1:T(2,128)}, u32[]{:S(2)}, u32[]{:S(2)}) %all-to-all-start) | async-done | bytes 8388640 | tf_op jit(solution)/shard_map/all_to_all | solution.py:35
  193.4 9.9 fusion.175
  203.2 5.9 fusion.11
  209.1 5.9 fusion.7
  215.0 6.1 convolution_add_fusion
  221.1 23.0 %subtract_bitcast_fusion.1 = (f32[1,32,32768]{2,1,0:T(8,128)S(1)}, f32[1,32,32768]{2,1,0:T(8,128)S(1)}) fusion(f32[32,32768]{1,0:T(8,128)S(1)} %convolution_add_fusion, s32[32768]{0:T(1024)S(1)} %iota_add_fusion, f32[32,32768]{1,0:T(8,128)S(1)} %fusion.11, f32[1,32,32768]{2,0,1:T(1,128)S(1)} %get-tuple-element.10), kind=kOutput, calls=%fused_computation.34 | convolution fusion | flops 424688640 | bytes 21102592 | tf_op jit(solution)/shard_map/dot_general | solution.py:18
  244.2 0.5 pad_maximum_fusion
  244.7 14.3 %copy.36 = f32[2,32,32768]{2,0,1:T(2,128)S(1)} copy(f32[2,32,32768]{2,1,0:T(8,128)S(1)} %pad_maximum_fusion) | data formatting | bytes 16777216 | tf_op jit(solution)/shard_map/stack | solution.py:64
  259.0 186.0 %all_to_all.15 = f32[2,32,32768]{2,0,1:T(2,128)} all-to-all(f32[2,32,32768]{2,0,1:T(2,128)S(1)} %copy.36), channel_id=1, replica_groups=mesh['hi'=4,'lo'=8] {'hi','lo'}, dimensions={1} | all-to-all | bytes 16777216 | tf_op jit(solution)/shard_map/all_to_all | solution.py:39
  445.0 28.8 %slice_reduce_fusion.1 = (f32[32,32768]{1,0:T(8,128)}, f32[32,32768]{1,0:T(8,128)}) fusion(f32[2,32,32768]{2,0,1:T(2,128)} %all_to_all.15), kind=kLoop, calls=%fused_computation.21 | loop fusion | bytes 16777216 | tf_op jit(solution)/shard_map/slice | solution.py:69
  473.8 4.9 squeeze.18
  478.8 4.9 squeeze.19
  483.7 31.5 %fusion.29 = f32[1024,1024]{1,0:T(8,128)S(1)} fusion(f32[1024,1024]{1,0:T(8,128)} %squeeze.19), kind=kOutput, calls=%fused_computation.53 | convolution fusion | flops 12900630528 | bytes 8388608 | tf_op jit(solution)/shard_map/dot_general | solution.py:18
  515.3 29.6 %fusion.30 = f32[1024,1024]{1,0:T(8,128)S(1)} fusion(f32[1024,1024]{1,0:T(8,128)S(1)} %copy-done), kind=kOutput, calls=%fused_computation.54 | convolution fusion | flops 12900630528 | bytes 8388608 | tf_op jit(solution)/shard_map/dot_general | solution.py:18
  544.9 29.2 %fusion.56 = f32[1024,1024]{1,0:T(8,128)S(1)} fusion(f32[1024,1024]{1,0:T(8,128)S(1)} %fusion.29, f32[1024,1024]{1,0:T(8,128)S(1)} %copy-done), kind=kOutput, calls=%fused_computation.72 | convolution fusion | flops 12901679104 | bytes 12582912 | tf_op jit(solution)/shard_map/dot_general | solution.py:18
  574.1 29.7 %fusion.55 = f32[1024,1024]{1,0:T(8,128)S(1)} fusion(f32[1024,1024]{1,0:T(8,128)S(1)} %fusion.30, f32[1024,1024]{1,0:T(8,128)S(1)} %copy-done.1), kind=kOutput, calls=%fused_computation.71 | convolution fusion | flops 12901679104 | bytes 12582912 | tf_op jit(solution)/shard_map/dot_general | solution.py:18
  603.8 16.8 %multiply_add_fusion.10 = f32[1024,1024]{1,0:T(8,128)S(1)} fusion(f32[1024,1024]{1,0:T(8,128)S(1)} %fusion.56, f32[1024,1024]{1,0:T(8,128)S(1)} %fusion.55), kind=kLoop, calls=%fused_computation.30.clone.clone.2 | loop fusion | flops 17825792 | bytes 12582912 | tf_op jit(solution)/shard_map/dot_general | solution.py:18
  620.7 16.8 %multiply_subtract_fusion.9 = f32[1024,1024]{1,0:T(8,128)S(1)} fusion(f32[1024,1024]{1,0:T(8,128)S(1)} %fusion.56, f32[1024,1024]{1,0:T(8,128)S(1)} %fusion.55), kind=kLoop, calls=%fused_computation.31.clone.clone.2 | loop fusion | flops 17825792 | bytes 12582912 | tf_op jit(solution)/shard_map/dot_general | solution.py:18
  637.5 16.8 %multiply_add_fusion.9 = f32[1024,1024]{1,0:T(8,128)S(1)} fusion(f32[1024,1024]{1,0:T(8,128)S(1)} %fusion.56, f32[1024,1024]{1,0:T(8,128)S(1)} %fusion.55), kind=kLoop, calls=%fused_computation.30.clone.1.clone.2 | loop fusion | flops 17825792 | bytes 12582912 | tf_op jit(solution)/shard_map/dot_general | solution.py:18
  654.3 16.8 %multiply_subtract_fusion.10 = f32[1024,1024]{1,0:T(8,128)S(1)} fusion(f32[1024,1024]{1,0:T(8,128)S(1)} %fusion.56, f32[1024,1024]{1,0:T(8,128)S(1)} %fusion.55), kind=kLoop, calls=%fused_computation.31.clone.1.clone.2 | loop fusion | flops 17825792 | bytes 12582912 | tf_op jit(solution)/shard_map/dot_general | solution.py:18
  671.2 31.3 %fusion.27 = f32[1024,1024]{1,0:T(8,128)S(1)} fusion(f32[1024,1024]{1,0:T(8,128)S(1)} %multiply_add_fusion.10), kind=kOutput, calls=%fused_computation.51 | convolution fusion | flops 12900630528 | bytes 8388608 | tf_op jit(solution)/shard_map/dot_general | solution.py:18
  702.5 31.4 %fusion.28 = f32[1024,1024]{1,0:T(8,128)S(1)} fusion(f32[1024,1024]{1,0:T(8,128)S(1)} %multiply_subtract_fusion.10), kind=kOutput, calls=%fused_computation.52 | convolution fusion | flops 12900630528 | bytes 8388608 | tf_op jit(solution)/shard_map/dot_general | solution.py:18
  733.9 31.5 %add_bitcast_fusion = f32[1,1024,1024]{2,1,0:T(8,128)S(1)} fusion(f32[1024,1024]{1,0:T(8,128)S(1)} %fusion.27, f32[1024,1024]{1,0:T(8,128)S(1)} %multiply_subtract_fusion.9), kind=kOutput, calls=%fused_computation.28 | convolution fusion | flops 12901679104 | bytes 12582912 | tf_op jit(solution)/shard_map/dot_general | solution.py:18
  765.4 31.3 %subtract_bitcast_fusion = f32[1,1024,1024]{2,1,0:T(8,128)S(1)} fusion(f32[1024,1024]{1,0:T(8,128)S(1)} %fusion.28, f32[1024,1024]{1,0:T(8,128)S(1)} %multiply_add_fusion.9), kind=kOutput, calls=%fused_computation.29 | convolution fusion | flops 12901679104 | bytes 12582912 | tf_op jit(solution)/shard_map/dot_general | solution.py:18
  796.7 4.2 maximum_bitcast_fusion
  800.9 8.7 copy.37
  809.6 9.5 reshape.25
  819.2 1.7 fusion.88
  820.9 1.8 fusion.87
  822.8 1.8 fusion.86
  824.6 1.8 fusion.85
  826.4 1.8 fusion.84
  828.3 1.8 fusion.83
  830.1 1.8 fusion.82
  831.9 1.8 fusion.81
  833.8 1.7 fusion.80
  835.5 1.8 fusion.79
  837.4 1.8 fusion.78
  839.2 1.8 fusion.77
  841.1 1.8 fusion.76
  842.9 1.8 fusion.75
  844.7 1.8 fusion.74
  846.6 1.8 fusion.73
  848.4 1.7 fusion.72
  850.2 1.8 fusion.71
  852.0 1.8 fusion.70
  853.9 1.8 fusion.69
  855.7 1.8 fusion.68
  857.5 1.8 fusion.67
  859.4 1.8 fusion.66
  861.2 1.8 fusion.65
  863.1 1.7 fusion.64
  864.8 1.8 fusion.63
  866.6 1.8 fusion.62
  868.5 1.8 fusion.61
  870.3 1.8 fusion.60
  872.2 1.8 fusion.59
  874.0 1.8 fusion.58
  875.9 1.8 fusion.57
  877.7 187.0 %all_to_all.16 = f32[32,2,1,32768]{3,2,1,0:T(1,128)S(1)} all-to-all(f32[32,2,1,32768]{3,2,1,0:T(1,128)S(1)} %fusion.57), channel_id=1, replica_groups=mesh['hi'=4,'lo'=8] {'hi','lo'}, dimensions={0} | all-to-all | bytes 16777216 | tf_op jit(solution)/shard_map/all_to_all | solution.py:13
  1064.7 7.6 copy.62
  1072.3 22.7 %copy.39 = f32[2,32768,32]{2,1,0:T(8,128)} copy(f32[2,32768,32]{1,0,2:T(2,128)} %bitcast.169) | data formatting | bytes 16777216 | tf_op jit(solution)/shard_map/transpose | solution.py:82
  1095.0 27.8 %reshape.28 = f32[2,1048576]{1,0:T(2,128)} reshape(f32[2,32768,32]{2,1,0:T(8,128)} %copy.39) | data formatting | bytes 16777216 | tf_op jit(solution)/shard_map/reshape | solution.py:82
  (5 shorter events, 0.0 us)
Async XLA Ops:
  0.0 193.4 %all-to-all-start = ((f32[2,32,32768]{2,0,1:T(2,128)}), f32[2,32,32768]{2,0,1:T(2,128)}, u32[]{:S(2)}, u32[]{:S(2)}) async-start(f32[2,32,32768]{2,0,1:T(2,128)} %bitcast.171), calls=%async_computation | async-start | bytes 16777216 | tf_op jit(solution)/shard_map/all_to_all | solution.py:35
  483.7 31.6 %copy-start = (f32[1024,1024]{1,0:T(8,128)S(1)}, f32[1024,1024]{1,0:T(8,128)}, u32[]{:S(2)}) copy-start(f32[1024,1024]{1,0:T(8,128)} %squeeze.18) | copy-start | bytes 12582916
  544.9 29.2 %copy-start.1 = (f32[1024,1024]{1,0:T(8,128)S(1)}, f32[1024,1024]{1,0:T(8,128)}, u32[]{:S(2)}) copy-start(f32[1024,1024]{1,0:T(8,128)} %squeeze.19) | copy-start | bytes 12582916
